TPU v7x, 256 devices: a whole 4x4x8 slice. The times are simulated.
256 devices in a mesh: layer: 16 (over y, x_hi, core), feat: 16 (over z, x_lo).
Axes of the slice: x: 4 (x_hi: 2, x_lo: 2; x = x_hi * 2 + x_lo), y: 4, z: 8, core: 2. Of those that a mesh axis runs over, the one named last changes fastest.
Arguments:
- residual_in: bfloat16 [16, 256, 4096], P('layer', None, 'feat'), may hold values from -6 to 6
- mlp_out: bfloat16 [16, 256, 4096], P('layer', None, 'feat'), may hold values from -6 to 6
- encoder: bfloat16 [16, 4096, 2048], P('layer', None, 'feat'), may hold values from -0.09375 to 0.09375
- encoder_bias: float32 [16, 2048], P('layer', 'feat'), may hold values from -3 to 3
- decoder: bfloat16 [16, 9, 2048, 4096], P('layer', None, 'feat'), may hold values from -0.046875 to 0.046875
- decoder_bias: float32 [16, 4096], P('layer'), may hold values from -3 to 3
Outputs:
- recon_error: bfloat16 [16, 256, 4096], P('layer', None, 'feat')
- pre_grad: float32 [16, 256, 2048], P('layer', None, 'feat')
All inputs are finite; a program needn't handle non-finite values.
Results may differ from a plain program's by a relative error of at most 0.0035.
Values may be sent and summed in bfloat16 or wider, within the bound.
A program may use at most 128 MiB of HBM per device.

v0:
```python
import jax
import jax.numpy as jnp
from jax import lax
from jax.sharding import Mesh
from jax.sharding import PartitionSpec as P

FEAT = ("feat_0", "feat_1")


def sent_to_all(array, axis):
    copies = jnp.broadcast_to(array, (lax.axis_size(axis), *array.shape))
    return lax.all_to_all(copies, axis, split_axis=0, concat_axis=0, tiled=True)


def joined_along(blocks, dim):
    shape = list(blocks.shape[1:])
    shape[dim] *= blocks.shape[0]
    return jnp.moveaxis(blocks, 0, dim).reshape(shape)


def collect(array, axis, dim):
    blocks = sent_to_all(array, axis)
    return joined_along(blocks, dim)


def scatter_axes(array, axes, dim):
    for axis in axes:
        array = lax.psum_scatter(array, axis, scatter_dimension=dim, tiled=True)
    return array


def swapped(array, axis, bit):
    return lax.ppermute(array, axis, [(i, i ^ 1 << bit) for i in range(lax.axis_size(axis))])


def sent_together(arrays, axis, dim, along):
    both = jnp.concatenate(arrays, axis=along)
    whole, at, outs = (lax.all_gather(both, axis, axis=dim, tiled=True), 0, [])
    for a in arrays:
        outs.append(lax.slice_in_dim(whole, at, at + a.shape[along], axis=along))
        at += a.shape[along]
    return tuple(outs)


def in_blocks(array, dim, peers):
    before, after = (array.shape[:dim], array.shape[dim + 1 :])
    return jnp.moveaxis(array.reshape(*before, peers, -1, *after), dim, 0)


def sum_at_owner(array, axis, dim):
    peers = lax.axis_size(axis)
    blocks = lax.all_to_all(in_blocks(array, dim, peers), axis, 0, 0, tiled=True)
    return jnp.sum(blocks, axis=0)


def placement_of(source, layer_row, half_layers, layers):
    own_flag = source <= jnp.minimum(layer_row, half_layers - 1)
    slot_index = jnp.where(own_flag, source, source - half_layers + layer_row + 1)
    over_flag = (
        jnp.logical_not(own_flag) & (source >= half_layers) & (source <= layers - 1 - layer_row)
    )
    return (slot_index, own_flag, over_flag)


def add_source(carry, code_rows, source, layer_row, half_layers, layers, weights):
    slot_index, own_flag, over_flag = placement_of(source, layer_row, half_layers, layers)

    def compute(inner):
        picked = jnp.clip(slot_index, 0, weights.shape[0] - 1)
        block = lax.dynamic_index_in_dim(weights, picked, 0, keepdims=False)
        product = jnp.dot(code_rows, block, preferred_element_type=jnp.float32)
        return (
            inner[0] + jnp.where(own_flag, product, 0.0),
            inner[1] + jnp.where(over_flag, product, 0.0),
        )

    def unchanged(inner):
        return inner

    return lax.cond(own_flag | over_flag, compute, unchanged, carry)


def shards(residual_in, mlp_out, encoder, encoder_bias, decoder, decoder_bias):
    layer_row = lax.axis_index("layer")
    layers = lax.axis_size("layer")
    half_layers = layers // 2
    weights = decoder[0]
    slot_count = weights.shape[0]
    enc_local = encoder[0]
    tokens = residual_in.shape[1]
    model_width = weights.shape[2]
    preact = jnp.dot(
        lax.all_gather(residual_in[0], FEAT, axis=1, tiled=True),
        enc_local,
        preferred_element_type=jnp.float32,
    )
    preact = preact + encoder_bias[0][None, :]
    codes = jnp.maximum(preact, 0.0).astype(jnp.bfloat16)
    empty = jnp.zeros((tokens, model_width), jnp.float32)
    piece = collect(codes[None], "layer", 0)

    def one_row(offset, inner):
        code_rows = lax.dynamic_index_in_dim(piece, offset, 0, keepdims=False)
        return add_source(inner, code_rows, offset, layer_row, half_layers, layers, weights)

    own_part, over_part = lax.fori_loop(0, piece.shape[0], one_row, (empty, empty))
    own_sum, over_sum = (scatter_axes(own_part, FEAT, 1), scatter_axes(over_part, FEAT, 1))
    hops = layers.bit_length() - 1
    for bit in range(hops):
        over_sum = swapped(over_sum, "layer", bit)
    column = lax.axis_index(FEAT)
    share_width = model_width // lax.axis_size(FEAT)
    bias_share = lax.dynamic_slice_in_dim(decoder_bias[0], column * share_width, share_width, 0)
    target_share = mlp_out[0].astype(jnp.float32)
    error_share = (own_sum + over_sum + bias_share[None, :] - target_share).astype(jnp.bfloat16)
    partner_share = error_share
    for bit in range(hops):
        partner_share = swapped(partner_share, "layer", bit)
    error_full, partner_full = sent_together((error_share, partner_share), FEAT, 1, 0)
    slot_ids = jnp.arange(slot_count, dtype=jnp.int32)
    own_slot = slot_ids <= jnp.minimum(layer_row, half_layers - 1)
    slot_errors = jnp.where(own_slot[:, None, None], error_full[None], partner_full[None])
    slot_terms = jnp.einsum(
        "jtd,jfd->jtf", slot_errors, weights, preferred_element_type=jnp.float32
    )
    sources = jnp.arange(layers, dtype=jnp.int32)
    slot_index, own_flag, over_flag = placement_of(sources, layer_row, half_layers, layers)
    picked = jnp.take(slot_terms, jnp.clip(slot_index, 0, slot_count - 1), axis=0)
    by_source = jnp.where((own_flag | over_flag)[:, None, None], picked, 0.0)
    back = sum_at_owner(by_source, "layer", 0)
    return (error_share[None], back)


def solution(mesh):
    split = Mesh(mesh.devices.reshape(mesh.shape["layer"], 8, 2), ("layer", "feat_0", "feat_1"))
    placed = (
        P("layer", None, FEAT),
        P("layer", None, FEAT),
        P("layer", None, FEAT),
        P("layer", FEAT),
        P("layer", None, FEAT, None),
        P("layer", None),
    )
    return jax.shard_map(
        shards,
        mesh=split,
        in_specs=placed,
        out_specs=(P("layer", None, FEAT), P("layer", None, FEAT)),
        check_vma=False,
    )
```

profile of v0, /device:TPU:2, one launch (start us, length us, event | category | flops | bytes accessed | tf_op | source)
XLA Modules:
  0.0 552.4 jit_solution(7001553876224597050)
XLA Ops:
  7.2 0.0 all-gather.6.cloned.1.call-start
  7.2 0.7 all-gather.6.cloned.1.call-update
  7.9 84.9 %all-gather.6.cloned.1.call-done = bf16[1,256,4096]{2,1,0:T(8,128)(2,1)} async-done(((bf16[1,256,256]{2,1,0:T(8,128)(2,1)}), bf16[1,256,4096]{2,1,0:T(8,128)(2,1)}) %all-gather.6.cloned.1.call-update) | async-done | bytes 2097168 | tf_op jit(solution)/shard_map/all_gather | solution.py:93
  92.8 2.3 fusion.21
  95.1 1.2 broadcast_in_dim.69
  96.3 7.7 %all-to-all-start = ((bf16[16,1,256,128]{3,2,1,0:T(8,128)(2,1)}), bf16[16,1,256,128]{3,2,1,0:T(8,128)(2,1)S(1)}, u32[]{:S(2)}, u32[]{:S(2)}) async-start(bf16[16,1,256,128]{3,2,1,0:T(8,128)(2,1)} %broadcast_in_dim.69), calls=%async_computation | async-start | bytes 2097152 | tf_op jit(solution)/shard_map/all_to_all | solution.py:12
  104.0 0.0 reduce-scatter.9.cloned.1.call-start
  104.1 18.0 %all-to-all-done = bf16[16,1,256,128]{3,2,1,0:T(8,128)(2,1)S(1)} async-done(((bf16[16,1,256,128]{3,2,1,0:T(8,128)(2,1)}), bf16[16,1,256,128]{3,2,1,0:T(8,128)(2,1)S(1)}, u32[]{:S(2)}, u32[]{:S(2)}) %all-to-all-start) | async-done | bytes 1048608 | tf_op jit(solution)/shard_map/all_to_all | solution.py:12
  122.1 2.4 broadcast_in_dim.68
  124.5 2.5 broadcast_in_dim.68.clone
  127.0 70.8 %while.17 = (s32[]{:T(128)}, f32[256,4096]{1,0:T(8,128)}, f32[256,4096]{1,0:T(8,128)}, s32[]{:T(128)}, s32[]{:T(128)}, /*index=5*/bf16[16,256,128]{2,1,0:T(8,128...) while((s32[]{:T(128)}, f32[256,4096]{1,0:T(8,128)}, f32[256,4096]{1,0:T(8,128)}, ...), condition=%wide.region_3.4_spmd, body=%wide.region_0.3_spmd.sunk | while | flops 272629760 | bytes 17892716 | solution.py:106
  127.0 7.9 %conditional.2 = ((f32[256,4096]{1,0:T(8,128)}, f32[256,4096]{1,0:T(8,128)})) conditional(s32[]{:T(128)} %convert_element_type.30, (f32[256,4096]{1,0:T(8,128)}, f32[256,4096]{1,0:T(8,128)}) %tuple.62, (pred[]{:T(512)}, s32[]{:T(128)}, bf16[16,256,128]{2,1,0:T(8,128)(2,1)S(1)}, s32[]{:T(128)}, bf16[9,128,4096]{2,1,0:T(8,128)(2,1)}, ...), branch_computations={%region_1.1_spmd, %region_2.2_spmd} | conditional | flops 272629760 | bytes 17892492 | solution.py:80
  127.0 7.9 %select_add_fusion = (f32[256,4096]{1,0:T(8,128)}, f32[256,4096]{1,0:T(8,128)}) fusion(f32[256,4096]{1,0:T(8,128)} %get-tuple-element.269, pred[]{:T(512)} %get-tuple-element.270, f32[256,4096]{1,0:T(8,128)} %get-tuple-element.263, pred[]{:T(512)} %get-tuple-element.264, bf16[9,128,4096]{2,1,0:T(8,128)(2,1)} %get-tuple-element.267, s32[]{:T(128)S(6)} %min.21, ...), kind=kOutput, calls=%fused_computation.1 | convolution fusion | flops 272629760 | bytes 17892360 | tf_op jit(solution)/shard_map/while/body/eval_jaxpr/cond/branch_1_fun/dot_general | solution.py:71
  134.9 7.9 %conditional.2 = ((f32[256,4096]{1,0:T(8,128)}, f32[256,4096]{1,0:T(8,128)})) conditional(s32[]{:T(128)} %convert_element_type.30, (f32[256,4096]{1,0:T(8,128)}, f32[256,4096]{1,0:T(8,128)}) %tuple.62, (pred[]{:T(512)}, s32[]{:T(128)}, bf16[16,256,128]{2,1,0:T(8,128)(2,1)S(1)}, s32[]{:T(128)}, bf16[9,128,4096]{2,1,0:T(8,128)(2,1)}, ...), branch_computations={%region_1.1_spmd, %region_2.2_spmd} | conditional | flops 272629760 | bytes 17892492 | solution.py:80
  135.0 7.9 %select_add_fusion = (f32[256,4096]{1,0:T(8,128)}, f32[256,4096]{1,0:T(8,128)}) fusion(f32[256,4096]{1,0:T(8,128)} %get-tuple-element.269, pred[]{:T(512)} %get-tuple-element.270, f32[256,4096]{1,0:T(8,128)} %get-tuple-element.263, pred[]{:T(512)} %get-tuple-element.264, bf16[9,128,4096]{2,1,0:T(8,128)(2,1)} %get-tuple-element.267, s32[]{:T(128)S(6)} %min.21, ...), kind=kOutput, calls=%fused_computation.1 | convolution fusion | flops 272629760 | bytes 17892360 | tf_op jit(solution)/shard_map/while/body/eval_jaxpr/cond/branch_1_fun/dot_general | solution.py:71
  142.8 7.9 %conditional.2 = ((f32[256,4096]{1,0:T(8,128)}, f32[256,4096]{1,0:T(8,128)})) conditional(s32[]{:T(128)} %convert_element_type.30, (f32[256,4096]{1,0:T(8,128)}, f32[256,4096]{1,0:T(8,128)}) %tuple.62, (pred[]{:T(512)}, s32[]{:T(128)}, bf16[16,256,128]{2,1,0:T(8,128)(2,1)S(1)}, s32[]{:T(128)}, bf16[9,128,4096]{2,1,0:T(8,128)(2,1)}, ...), branch_computations={%region_1.1_spmd, %region_2.2_spmd} | conditional | flops 272629760 | bytes 17892492 | solution.py:80
  142.8 7.8 %select_add_fusion = (f32[256,4096]{1,0:T(8,128)}, f32[256,4096]{1,0:T(8,128)}) fusion(f32[256,4096]{1,0:T(8,128)} %get-tuple-element.269, pred[]{:T(512)} %get-tuple-element.270, f32[256,4096]{1,0:T(8,128)} %get-tuple-element.263, pred[]{:T(512)} %get-tuple-element.264, bf16[9,128,4096]{2,1,0:T(8,128)(2,1)} %get-tuple-element.267, s32[]{:T(128)S(6)} %min.21, ...), kind=kOutput, calls=%fused_computation.1 | convolution fusion | flops 272629760 | bytes 17892360 | tf_op jit(solution)/shard_map/while/body/eval_jaxpr/cond/branch_1_fun/dot_general | solution.py:71
  150.7 7.9 %conditional.2 = ((f32[256,4096]{1,0:T(8,128)}, f32[256,4096]{1,0:T(8,128)})) conditional(s32[]{:T(128)} %convert_element_type.30, (f32[256,4096]{1,0:T(8,128)}, f32[256,4096]{1,0:T(8,128)}) %tuple.62, (pred[]{:T(512)}, s32[]{:T(128)}, bf16[16,256,128]{2,1,0:T(8,128)(2,1)S(1)}, s32[]{:T(128)}, bf16[9,128,4096]{2,1,0:T(8,128)(2,1)}, ...), branch_computations={%region_1.1_spmd, %region_2.2_spmd} | conditional | flops 272629760 | bytes 17892492 | solution.py:80
  150.7 7.9 %select_add_fusion = (f32[256,4096]{1,0:T(8,128)}, f32[256,4096]{1,0:T(8,128)}) fusion(f32[256,4096]{1,0:T(8,128)} %get-tuple-element.269, pred[]{:T(512)} %get-tuple-element.270, f32[256,4096]{1,0:T(8,128)} %get-tuple-element.263, pred[]{:T(512)} %get-tuple-element.264, bf16[9,128,4096]{2,1,0:T(8,128)(2,1)} %get-tuple-element.267, s32[]{:T(128)S(6)} %min.21, ...), kind=kOutput, calls=%fused_computation.1 | convolution fusion | flops 272629760 | bytes 17892360 | tf_op jit(solution)/shard_map/while/body/eval_jaxpr/cond/branch_1_fun/dot_general | solution.py:71
  158.5 7.9 %conditional.2 = ((f32[256,4096]{1,0:T(8,128)}, f32[256,4096]{1,0:T(8,128)})) conditional(s32[]{:T(128)} %convert_element_type.30, (f32[256,4096]{1,0:T(8,128)}, f32[256,4096]{1,0:T(8,128)}) %tuple.62, (pred[]{:T(512)}, s32[]{:T(128)}, bf16[16,256,128]{2,1,0:T(8,128)(2,1)S(1)}, s32[]{:T(128)}, bf16[9,128,4096]{2,1,0:T(8,128)(2,1)}, ...), branch_computations={%region_1.1_spmd, %region_2.2_spmd} | conditional | flops 272629760 | bytes 17892492 | solution.py:80
  158.5 7.8 %select_add_fusion = (f32[256,4096]{1,0:T(8,128)}, f32[256,4096]{1,0:T(8,128)}) fusion(f32[256,4096]{1,0:T(8,128)} %get-tuple-element.269, pred[]{:T(512)} %get-tuple-element.270, f32[256,4096]{1,0:T(8,128)} %get-tuple-element.263, pred[]{:T(512)} %get-tuple-element.264, bf16[9,128,4096]{2,1,0:T(8,128)(2,1)} %get-tuple-element.267, s32[]{:T(128)S(6)} %min.21, ...), kind=kOutput, calls=%fused_computation.1 | convolution fusion | flops 272629760 | bytes 17892360 | tf_op jit(solution)/shard_map/while/body/eval_jaxpr/cond/branch_1_fun/dot_general | solution.py:71
  166.4 7.9 %conditional.2 = ((f32[256,4096]{1,0:T(8,128)}, f32[256,4096]{1,0:T(8,128)})) conditional(s32[]{:T(128)} %convert_element_type.30, (f32[256,4096]{1,0:T(8,128)}, f32[256,4096]{1,0:T(8,128)}) %tuple.62, (pred[]{:T(512)}, s32[]{:T(128)}, bf16[16,256,128]{2,1,0:T(8,128)(2,1)S(1)}, s32[]{:T(128)}, bf16[9,128,4096]{2,1,0:T(8,128)(2,1)}, ...), branch_computations={%region_1.1_spmd, %region_2.2_spmd} | conditional | flops 272629760 | bytes 17892492 | solution.py:80
  166.4 7.9 %select_add_fusion = (f32[256,4096]{1,0:T(8,128)}, f32[256,4096]{1,0:T(8,128)}) fusion(f32[256,4096]{1,0:T(8,128)} %get-tuple-element.269, pred[]{:T(512)} %get-tuple-element.270, f32[256,4096]{1,0:T(8,128)} %get-tuple-element.263, pred[]{:T(512)} %get-tuple-element.264, bf16[9,128,4096]{2,1,0:T(8,128)(2,1)} %get-tuple-element.267, s32[]{:T(128)S(6)} %min.21, ...), kind=kOutput, calls=%fused_computation.1 | convolution fusion | flops 272629760 | bytes 17892360 | tf_op jit(solution)/shard_map/while/body/eval_jaxpr/cond/branch_1_fun/dot_general | solution.py:71
  174.2 7.9 %conditional.2 = ((f32[256,4096]{1,0:T(8,128)}, f32[256,4096]{1,0:T(8,128)})) conditional(s32[]{:T(128)} %convert_element_type.30, (f32[256,4096]{1,0:T(8,128)}, f32[256,4096]{1,0:T(8,128)}) %tuple.62, (pred[]{:T(512)}, s32[]{:T(128)}, bf16[16,256,128]{2,1,0:T(8,128)(2,1)S(1)}, s32[]{:T(128)}, bf16[9,128,4096]{2,1,0:T(8,128)(2,1)}, ...), branch_computations={%region_1.1_spmd, %region_2.2_spmd} | conditional | flops 272629760 | bytes 17892492 | solution.py:80
  174.2 7.8 %select_add_fusion = (f32[256,4096]{1,0:T(8,128)}, f32[256,4096]{1,0:T(8,128)}) fusion(f32[256,4096]{1,0:T(8,128)} %get-tuple-element.269, pred[]{:T(512)} %get-tuple-element.270, f32[256,4096]{1,0:T(8,128)} %get-tuple-element.263, pred[]{:T(512)} %get-tuple-element.264, bf16[9,128,4096]{2,1,0:T(8,128)(2,1)} %get-tuple-element.267, s32[]{:T(128)S(6)} %min.21, ...), kind=kOutput, calls=%fused_computation.1 | convolution fusion | flops 272629760 | bytes 17892360 | tf_op jit(solution)/shard_map/while/body/eval_jaxpr/cond/branch_1_fun/dot_general | solution.py:71
  182.1 7.9 %conditional.2 = ((f32[256,4096]{1,0:T(8,128)}, f32[256,4096]{1,0:T(8,128)})) conditional(s32[]{:T(128)} %convert_element_type.30, (f32[256,4096]{1,0:T(8,128)}, f32[256,4096]{1,0:T(8,128)}) %tuple.62, (pred[]{:T(512)}, s32[]{:T(128)}, bf16[16,256,128]{2,1,0:T(8,128)(2,1)S(1)}, s32[]{:T(128)}, bf16[9,128,4096]{2,1,0:T(8,128)(2,1)}, ...), branch_computations={%region_1.1_spmd, %region_2.2_spmd} | conditional | flops 272629760 | bytes 17892492 | solution.py:80
  182.1 7.9 %select_add_fusion = (f32[256,4096]{1,0:T(8,128)}, f32[256,4096]{1,0:T(8,128)}) fusion(f32[256,4096]{1,0:T(8,128)} %get-tuple-element.269, pred[]{:T(512)} %get-tuple-element.270, f32[256,4096]{1,0:T(8,128)} %get-tuple-element.263, pred[]{:T(512)} %get-tuple-element.264, bf16[9,128,4096]{2,1,0:T(8,128)(2,1)} %get-tuple-element.267, s32[]{:T(128)S(6)} %min.21, ...), kind=kOutput, calls=%fused_computation.1 | convolution fusion | flops 272629760 | bytes 17892360 | tf_op jit(solution)/shard_map/while/body/eval_jaxpr/cond/branch_1_fun/dot_general | solution.py:71
  189.9 7.9 %conditional.2 = ((f32[256,4096]{1,0:T(8,128)}, f32[256,4096]{1,0:T(8,128)})) conditional(s32[]{:T(128)} %convert_element_type.30, (f32[256,4096]{1,0:T(8,128)}, f32[256,4096]{1,0:T(8,128)}) %tuple.62, (pred[]{:T(512)}, s32[]{:T(128)}, bf16[16,256,128]{2,1,0:T(8,128)(2,1)S(1)}, s32[]{:T(128)}, bf16[9,128,4096]{2,1,0:T(8,128)(2,1)}, ...), branch_computations={%region_1.1_spmd, %region_2.2_spmd} | conditional | flops 272629760 | bytes 17892492 | solution.py:80
  189.9 7.8 %select_add_fusion = (f32[256,4096]{1,0:T(8,128)}, f32[256,4096]{1,0:T(8,128)}) fusion(f32[256,4096]{1,0:T(8,128)} %get-tuple-element.269, pred[]{:T(512)} %get-tuple-element.270, f32[256,4096]{1,0:T(8,128)} %get-tuple-element.263, pred[]{:T(512)} %get-tuple-element.264, bf16[9,128,4096]{2,1,0:T(8,128)(2,1)} %get-tuple-element.267, s32[]{:T(128)S(6)} %min.21, ...), kind=kOutput, calls=%fused_computation.1 | convolution fusion | flops 272629760 | bytes 17892360 | tf_op jit(solution)/shard_map/while/body/eval_jaxpr/cond/branch_1_fun/dot_general | solution.py:71
  197.8 0.0 reduce-scatter.9.cloned.1.call-update
  197.8 0.0 reduce-scatter.11.cloned.1.call-start
  197.9 51.0 %reduce-scatter.9.cloned.1.call-done = f32[256,512]{1,0:T(8,128)} async-done(((f32[256,4096]{1,0:T(8,128)}), f32[256,512]{1,0:T(8,128)}) %reduce-scatter.9.cloned.1.call-update) | async-done | bytes 524304 | tf_op jit(solution)/shard_map/reduce_scatter | solution.py:28
  248.9 0.0 reduce-scatter.11.cloned.1.call-update
  248.9 0.0 reduce-scatter.5.cloned.1.call-start
  249.0 0.5 reduce-scatter.5.cloned.1.call-update
  249.5 0.0 reduce-scatter.7.cloned.1.call-start
  249.5 19.1 %reduce-scatter.11.cloned.1.call-done = f32[256,256]{1,0:T(8,128)} async-done(((f32[256,512]{1,0:T(8,128)}), f32[256,256]{1,0:T(8,128)}) %reduce-scatter.11.cloned.1.call-update) | async-done | bytes 262160 | tf_op jit(solution)/shard_map/reduce_scatter | solution.py:28
  268.7 59.9 %reduce-scatter.5.cloned.1.call-done = f32[256,512]{1,0:T(8,128)} async-done(((f32[256,4096]{1,0:T(8,128)}), f32[256,512]{1,0:T(8,128)}) %reduce-scatter.5.cloned.1.call-update) | async-done | bytes 524304 | tf_op jit(solution)/shard_map/reduce_scatter | solution.py:28
  328.6 0.0 all-gather.4.cloned.1.call-start
  328.6 2.2 collective-permute-start.1
  330.8 7.4 %collective-permute-done.1 = f32[256,256]{1,0:T(8,128)S(1)} collective-permute-done((f32[256,256]{1,0:T(8,128)S(1)}, f32[256,256]{1,0:T(8,128)S(1)}, u32[]{:S(2)}, u32[]{:S(2)}) %collective-permute-start.1) | collective-permute-done | bytes 262176 | tf_op jit(solution)/shard_map/ppermute | solution.py:33
  338.2 1.5 collective-permute-start.2
  339.7 5.6 %collective-permute-done.2 = f32[256,256]{1,0:T(8,128)S(1)} collective-permute-done((f32[256,256]{1,0:T(8,128)S(1)}, f32[256,256]{1,0:T(8,128)S(1)}, u32[]{:S(2)}, u32[]{:S(2)}) %collective-permute-start.2) | collective-permute-done | bytes 262176 | tf_op jit(solution)/shard_map/ppermute | solution.py:33
  345.3 3.0 collective-permute-start.3
  348.3 0.7 constant_dynamic-slice_fusion
  349.0 4.2 collective-permute-done.3
  353.2 1.0 fusion.25
  354.2 0.1 collective-permute-start.4
  354.3 1.3 collective-permute-done.4
  355.6 2.1 collective-permute-start.5
  357.7 5.0 collective-permute-done.5
  362.7 1.5 collective-permute-start.6
  364.2 3.5 collective-permute-done.6
  367.7 3.0 collective-permute-start.7
  370.7 3.5 collective-permute-done.7
  374.1 0.7 pad_maximum_fusion
  374.9 0.0 all-gather.4.cloned.1.call-update
  375.0 118.1 %all-gather.4.cloned.1.call-done = bf16[512,4096]{1,0:T(8,128)(2,1)} async-done(((bf16[512,256]{1,0:T(8,128)(2,1)}), bf16[512,4096]{1,0:T(8,128)(2,1)}) %all-gather.4.cloned.1.call-update) | async-done | bytes 4194320 | tf_op jit(solution)/shard_map/all_gather | solution.py:38
  493.1 2.7 fusion.30
  495.8 8.8 %fusion.6 = f32[9,256,128]{2,1,0:T(8,128)} fusion(pred[9]{0:T(512)(128)(4,1)S(1)} %iota_compare_fusion, bf16[256,4096]{1,0:T(8,128)(2,1)S(1)} %get-tuple-element.307, bf16[256,4096]{1,0:T(8,128)(2,1)S(1)} %get-tuple-element.306, bf16[1,9,128,4096]{3,2,1,0:T(8,128)(2,1)} %bitcast.44), kind=kOutput, calls=%fused_computation.9 | convolution fusion | flops 2425356288 | bytes 14811145 | tf_op jit(solution)/shard_map/jtd,jfd->jtf/dot_general | solution.py:123
  504.6 1.9 gather_fusion
  506.6 0.3 fusion.12
  506.9 37.9 %all_to_all.10 = f32[16,1,256,128]{3,2,1,0:T(8,128)S(1)} all-to-all(f32[16,1,256,128]{3,2,1,0:T(8,128)S(1)} %fusion.12), channel_id=1, replica_groups=mesh['layer'=16,'feat_0'=8,'feat_1'=2] {'layer'}, dimensions={0} | all-to-all | bytes 4194304 | tf_op jit(solution)/shard_map/all_to_all | solution.py:52
  544.8 0.8 reduce_sum.11
  (21 shorter events, 0.1 us)
Async XLA Ops:
  7.2 85.6 %copy-start = (bf16[1,4096,128]{2,1,0:T(8,128)(2,1)S(1)}, bf16[1,4096,128]{2,1,0:T(8,128)(2,1)}, u32[]{:S(2)}) copy-start(bf16[1,4096,128]{2,1,0:T(8,128)(2,1)} %param.12) | copy-start | bytes 3145732
  7.2 85.6 %all-gather.6.cloned.1.call-start = ((), (), s32[]{:S(2)}) async-start(), calls=%async_computation.11 | async-start | bytes 2228224 | tf_op jit(solution)/shard_map/all_gather | solution.py:93
  96.3 25.8 %all-to-all-start = ((bf16[16,1,256,128]{3,2,1,0:T(8,128)(2,1)}), bf16[16,1,256,128]{3,2,1,0:T(8,128)(2,1)S(1)}, u32[]{:S(2)}, u32[]{:S(2)}) async-start(bf16[16,1,256,128]{3,2,1,0:T(8,128)(2,1)} %broadcast_in_dim.69), calls=%async_computation | async-start | bytes 2097152 | tf_op jit(solution)/shard_map/all_to_all | solution.py:12
  104.0 144.9 %reduce-scatter.9.cloned.1.call-start = ((), (), s32[]{:S(2)}) async-start(), calls=%async_computation.8 | async-start | bytes 4718592 | tf_op jit(solution)/shard_map/reduce_scatter | solution.py:28
  197.8 155.4 %copy-start.2 = (bf16[1,256,256]{2,1,0:T(8,128)(2,1)S(1)}, bf16[1,256,256]{2,1,0:T(8,128)(2,1)}, u32[]{:S(2)}) copy-start(bf16[1,256,256]{2,1,0:T(8,128)(2,1)} %param.11) | copy-start | bytes 393220
  197.8 70.9 %reduce-scatter.11.cloned.1.call-start = ((), (), s32[]{:S(2)}) async-start(), calls=%async_computation.9 | async-start | bytes 786432 | tf_op jit(solution)/shard_map/reduce_scatter | solution.py:28
  248.9 79.6 %reduce-scatter.5.cloned.1.call-start = ((), (), s32[]{:S(2)}) async-start(), calls=%async_computation.6 | async-start | bytes 4718592 | tf_op jit(solution)/shard_map/reduce_scatter | solution.py:28
  249.5 99.5 %reduce-scatter.7.cloned.1.call-start = ((), (), s32[]{:S(2)}) async-start(), calls=%async_computation.7 | async-start | bytes 786432 | tf_op jit(solution)/shard_map/reduce_scatter | solution.py:28
  268.7 59.9 %collective-permute-start = (f32[256,256]{1,0:T(8,128)}, f32[256,256]{1,0:T(8,128)S(1)}, u32[]{:S(2)}, u32[]{:S(2)}) collective-permute-start(f32[256,256]{1,0:T(8,128)} %reduce-scatter.11.cloned.1.call-done), channel_id=1, source_target_pairs={{0,16},{16,0},{32,48},{48,32},{64,80},{80,64},{96,112},{112,96},{1... | collective-permute-start | bytes 786440 | tf_op jit(solution)/shard_map/ppermute | solution.py:33
  328.6 164.5 %all-gather.4.cloned.1.call-start = ((), (), s32[]{:S(2)}) async-start(), calls=%async_computation.10 | async-start | bytes 4456448 | tf_op jit(solution)/shard_map/all_gather | solution.py:38
  328.6 9.6 %collective-permute-start.1 = (f32[256,256]{1,0:T(8,128)S(1)}, f32[256,256]{1,0:T(8,128)S(1)}, u32[]{:S(2)}, u32[]{:S(2)}) collective-permute-start(f32[256,256]{1,0:T(8,128)S(1)} %collective-permute-done), channel_id=1, source_target_pairs={{0,32},{16,48},{32,0},{48,16},{64,96},{80,112},{96,64},{112,80},{1... | collective-permute-start | bytes 786440 | tf_op jit(solution)/shard_map/ppermute | solution.py:33
  338.2 7.1 %collective-permute-start.2 = (f32[256,256]{1,0:T(8,128)S(1)}, f32[256,256]{1,0:T(8,128)S(1)}, u32[]{:S(2)}, u32[]{:S(2)}) collective-permute-start(f32[256,256]{1,0:T(8,128)S(1)} %collective-permute-done.1), channel_id=1, source_target_pairs={{0,64},{16,80},{32,96},{48,112},{64,0},{80,16},{96,32},{112,48},{1... | collective-permute-start | bytes 786440 | tf_op jit(solution)/shard_map/ppermute | solution.py:33
  345.3 7.9 %collective-permute-start.3 = (f32[256,256]{1,0:T(8,128)S(1)}, f32[256,256]{1,0:T(8,128)S(1)}, u32[]{:S(2)}, u32[]{:S(2)}) collective-permute-start(f32[256,256]{1,0:T(8,128)S(1)} %collective-permute-done.2), channel_id=1, source_target_pairs={{0,128},{16,144},{32,160},{48,176},{64,192},{80,208},{96,224},{112... | collective-permute-start | bytes 786440 | tf_op jit(solution)/shard_map/ppermute | solution.py:33
  354.2 141.6 %copy-start.1 = (bf16[256,256]{1,0:T(8,128)(2,1)}, bf16[256,256]{1,0:T(8,128)(2,1)S(1)}, u32[]{:S(2)}) copy-start(bf16[256,256]{1,0:T(8,128)(2,1)S(1)} %fusion.25) | copy-start | bytes 393220
  354.2 1.4 collective-permute-start.4
  355.6 7.1 %collective-permute-start.5 = (bf16[256,256]{1,0:T(8,128)(2,1)S(1)}, bf16[256,256]{1,0:T(8,128)(2,1)S(1)}, u32[]{:S(2)}, u32[]{:S(2)}) collective-permute-start(bf16[256,256]{1,0:T(8,128)(2,1)S(1)} %collective-permute-done.4), channel_id=1, source_target_pairs={{0,32},{16,48},{32,0},{48,16},{64,96},{80,112},{96,64},{112,80},{1... | collective-permute-start | bytes 393224 | tf_op jit(solution)/shard_map/ppermute | solution.py:33
  362.7 5.0 collective-permute-start.6
  367.7 6.5 %collective-permute-start.7 = (bf16[256,256]{1,0:T(8,128)(2,1)S(1)}, bf16[256,256]{1,0:T(8,128)(2,1)S(1)}, u32[]{:S(2)}, u32[]{:S(2)}) collective-permute-start(bf16[256,256]{1,0:T(8,128)(2,1)S(1)} %collective-permute-done.6), channel_id=1, source_target_pairs={{0,128},{16,144},{32,160},{48,176},{64,192},{80,208},{96,224},{112... | collective-permute-start | bytes 393224 | tf_op jit(solution)/shard_map/ppermute | solution.py:33
Sparse Core Ops, SparseCore 0:
  9.7 83.0 all-gather.5
  197.9 50.9 reduce-scatter.8
  251.4 17.2 reduce-scatter.10
  271.1 57.4 reduce-scatter.4
  330.9 17.2 reduce-scatter.6
  375.0 118.0 all-gather.3
where the time goes:
time: 553 us; the launch traced here: 552 us
  waiting for transfers between devices  383 us (69%)
  matrix products  81.8 us (15%)
  blocking collectives  37.9 us (7%)
  starting transfers between devices  21.3 us (4%)
  between operations  14.2 us (3%)
  local copies, waits for them, and re-layouts  11.5 us (2%)
    reduce_scatter x4, waiting for transfers between devices, scatter_axes(): array = lax.psum_scatter(array, axis, scatter_dimension=dim, tiled=True)  130 us
    all_gather x1, waiting for transfers between devices, sent_together(): whole, at, outs = (lax.all_gather(both, axis, axis=dim, tiled=True), 0, [])  118 us
    all_gather x1, waiting for transfers between devices, shards(): lax.all_gather(residual_in[0], FEAT, axis=1, tiled=True)  84.9 us
    dot_general x9, matrix products, compute(): product = jnp.dot(code_rows, block, preferred_element_type=jnp.float32)  70.7 us
    all_to_all x1, blocking collectives, sum_at_owner(): lax.all_to_all(in_blocks(array, dim, peers), axis, 0, 0, tiled=True)  37.9 us
    ppermute x8, waiting for transfers between devices, swapped(): lax.ppermute(array, axis, [(i, i ^ 1 << bit) for i in range(lax.axis_size...  30.5 us
    all_to_all x1, waiting for transfers between devices, sent_to_all(): return lax.all_to_all(copies, axis, split_axis=0, concat_axis=0, tiled=True)  18 us
    ppermute x8, starting transfers between devices, swapped(): lax.ppermute(array, axis, [(i, i ^ 1 << bit) for i in range(lax.axis_size...  13.3 us
  transfers between devices with their start and end apart: 15, of which 13 were waited for; matrix products, arithmetic and copies ran while one was open for 0% of the time, Pallas kernels for 0%

commit v1 on v0

--- a/solution.py
+++ b/solution.py
@@ -90,7 +90,9 @@
     tokens = residual_in.shape[1]
     model_width = weights.shape[2]
     preact = jnp.dot(
-        lax.all_gather(residual_in[0], FEAT, axis=1, tiled=True),
+        jnp.concatenate(
+            lax.all_to_all(jnp.stack([residual_in[0]] * lax.axis_size(FEAT)), FEAT, 0, 0), axis=1
+        ),
         enc_local,
         preferred_element_type=jnp.float32,
     )

time: 553 us -> 523 us (0.946)
  waiting for transfers between devices: 383 us -> 296 us
  blocking collectives: 37.9 us -> 96.6 us
    all_gather x1 -> x0, waiting for transfers between devices: 84.9 us -> none  [shards(): lax.all_gather(residual_in[0], FEAT, axis=1, tiled=True)]
    all_to_all x0 -> x1, blocking collectives: none -> 58.7 us  [shards(): lax.all_to_all(jnp.stack([residual_in[0]] * lax.axis_size(FEAT)), FEAT, 0...]
  transfers between devices with their start and end apart: 15 -> 14, of which waited for: 13 -> 12; matrix products, arithmetic and copies ran while one was open for 0% -> 0% of each run, Pallas kernels for 0% -> 0%
where the time goes in v1:
time: 523 us; the launch traced here: 522 us
  waiting for transfers between devices  296 us (57%)
  blocking collectives  96.6 us (18%)
  matrix products  80 us (15%)
  starting transfers between devices  19.7 us (4%)
  between operations  13.9 us (3%)
  local copies, waits for them, and re-layouts  12.7 us (2%)
    reduce_scatter x4, waiting for transfers between devices, scatter_axes(): array = lax.psum_scatter(array, axis, scatter_dimension=dim, tiled=True)  129 us
    all_gather x1, waiting for transfers between devices, sent_together(): whole, at, outs = (lax.all_gather(both, axis, axis=dim, tiled=True), 0, [])  118 us
    dot_general x9, matrix products, compute(): product = jnp.dot(code_rows, block, preferred_element_type=jnp.float32)  70.4 us
    all_to_all x1, blocking collectives, shards(): lax.all_to_all(jnp.stack([residual_in[0]] * lax.axis_size(FEAT)), FEAT, 0...  58.7 us
    all_to_all x1, blocking collectives, sum_at_owner(): lax.all_to_all(in_blocks(array, dim, peers), axis, 0, 0, tiled=True)  37.9 us
    ppermute x8, waiting for transfers between devices, swapped(): lax.ppermute(array, axis, [(i, i ^ 1 << bit) for i in range(lax.axis_size...  30.5 us
    all_to_all x1, waiting for transfers between devices, sent_to_all(): return lax.all_to_all(copies, axis, split_axis=0, concat_axis=0, tiled=True)  18 us
    ppermute x8, starting transfers between devices, swapped(): lax.ppermute(array, axis, [(i, i ^ 1 << bit) for i in range(lax.axis_size...  13.3 us
  transfers between devices with their start and end apart: 14, of which 12 were waited for; matrix products, arithmetic and copies ran while one was open for 0% of the time, Pallas kernels for 0%

profile of v1, /device:TPU:2, one launch (start us, length us, event | category | flops | bytes accessed | tf_op | source)
XLA Modules:
  0.0 522.1 jit_solution(14417106080039029459)
XLA Ops:
  7.2 1.1 copy.9
  8.3 0.2 stack.3
  8.5 58.7 %all_to_all.15 = bf16[16,256,256]{1,2,0:T(8,128)(2,1)S(1)} all-to-all(bf16[16,256,256]{1,2,0:T(8,128)(2,1)S(1)} %stack.3), channel_id=1, replica_groups=mesh['layer'=16,'feat_0'=8,'feat_1'=2] {'feat_0','feat_1'}, dimensions={0} | all-to-all | bytes 4194304 | tf_op jit(solution)/shard_map/all_to_all | solution.py:94
  67.2 0.8 fusion.14
  67.9 1.2 broadcast_in_dim.69
  69.1 6.1 %all-to-all-start.1 = ((bf16[16,1,256,128]{3,2,1,0:T(8,128)(2,1)}), bf16[16,1,256,128]{3,2,1,0:T(8,128)(2,1)S(1)}, u32[]{:S(2)}, u32[]{:S(2)}) async-start(bf16[16,1,256,128]{3,2,1,0:T(8,128)(2,1)} %broadcast_in_dim.69), calls=%async_computation.1 | async-start | bytes 2097152 | tf_op jit(solution)/shard_map/all_to_all | solution.py:12
  75.3 0.0 reduce-scatter.9.cloned.1.call-start
  75.3 18.0 %all-to-all-done.1 = bf16[16,1,256,128]{3,2,1,0:T(8,128)(2,1)S(1)} async-done(((bf16[16,1,256,128]{3,2,1,0:T(8,128)(2,1)}), bf16[16,1,256,128]{3,2,1,0:T(8,128)(2,1)S(1)}, u32[]{:S(2)}, u32[]{:S(2)}) %all-to-all-start.1) | async-done | bytes 1048608 | tf_op jit(solution)/shard_map/all_to_all | solution.py:12
  93.3 2.4 broadcast_in_dim.68
  95.7 2.5 broadcast_in_dim.68.clone
  98.2 70.6 %while.17 = (s32[]{:T(128)}, f32[256,4096]{1,0:T(8,128)}, f32[256,4096]{1,0:T(8,128)}, s32[]{:T(128)}, s32[]{:T(128)}, /*index=5*/bf16[16,256,128]{2,1,0:T(8,128...) while((s32[]{:T(128)}, f32[256,4096]{1,0:T(8,128)}, f32[256,4096]{1,0:T(8,128)}, ...), condition=%wide.region_3.4_spmd, body=%wide.region_0.3_spmd.sunk | while | flops 272629760 | bytes 17892716 | solution.py:108
  98.2 7.8 %conditional.2 = ((f32[256,4096]{1,0:T(8,128)}, f32[256,4096]{1,0:T(8,128)})) conditional(s32[]{:T(128)} %convert_element_type.30, (f32[256,4096]{1,0:T(8,128)}, f32[256,4096]{1,0:T(8,128)}) %tuple.62, (pred[]{:T(512)}, s32[]{:T(128)}, bf16[16,256,128]{2,1,0:T(8,128)(2,1)S(1)}, s32[]{:T(128)}, bf16[9,128,4096]{2,1,0:T(8,128)(2,1)}, ...), branch_computations={%region_1.1_spmd, %region_2.2_spmd} | conditional | flops 272629760 | bytes 17892492 | solution.py:80
  98.2 7.8 %select_add_fusion = (f32[256,4096]{1,0:T(8,128)}, f32[256,4096]{1,0:T(8,128)}) fusion(f32[256,4096]{1,0:T(8,128)} %get-tuple-element.269, pred[]{:T(512)} %get-tuple-element.270, f32[256,4096]{1,0:T(8,128)} %get-tuple-element.263, pred[]{:T(512)} %get-tuple-element.264, bf16[9,128,4096]{2,1,0:T(8,128)(2,1)} %get-tuple-element.267, s32[]{:T(128)S(6)} %min.21, ...), kind=kOutput, calls=%fused_computation.1 | convolution fusion | flops 272629760 | bytes 17892360 | tf_op jit(solution)/shard_map/while/body/eval_jaxpr/cond/branch_1_fun/dot_general | solution.py:71
  106.1 7.9 %conditional.2 = ((f32[256,4096]{1,0:T(8,128)}, f32[256,4096]{1,0:T(8,128)})) conditional(s32[]{:T(128)} %convert_element_type.30, (f32[256,4096]{1,0:T(8,128)}, f32[256,4096]{1,0:T(8,128)}) %tuple.62, (pred[]{:T(512)}, s32[]{:T(128)}, bf16[16,256,128]{2,1,0:T(8,128)(2,1)S(1)}, s32[]{:T(128)}, bf16[9,128,4096]{2,1,0:T(8,128)(2,1)}, ...), branch_computations={%region_1.1_spmd, %region_2.2_spmd} | conditional | flops 272629760 | bytes 17892492 | solution.py:80
  106.2 7.8 %select_add_fusion = (f32[256,4096]{1,0:T(8,128)}, f32[256,4096]{1,0:T(8,128)}) fusion(f32[256,4096]{1,0:T(8,128)} %get-tuple-element.269, pred[]{:T(512)} %get-tuple-element.270, f32[256,4096]{1,0:T(8,128)} %get-tuple-element.263, pred[]{:T(512)} %get-tuple-element.264, bf16[9,128,4096]{2,1,0:T(8,128)(2,1)} %get-tuple-element.267, s32[]{:T(128)S(6)} %min.21, ...), kind=kOutput, calls=%fused_computation.1 | convolution fusion | flops 272629760 | bytes 17892360 | tf_op jit(solution)/shard_map/while/body/eval_jaxpr/cond/branch_1_fun/dot_general | solution.py:71
  114.0 7.8 %conditional.2 = ((f32[256,4096]{1,0:T(8,128)}, f32[256,4096]{1,0:T(8,128)})) conditional(s32[]{:T(128)} %convert_element_type.30, (f32[256,4096]{1,0:T(8,128)}, f32[256,4096]{1,0:T(8,128)}) %tuple.62, (pred[]{:T(512)}, s32[]{:T(128)}, bf16[16,256,128]{2,1,0:T(8,128)(2,1)S(1)}, s32[]{:T(128)}, bf16[9,128,4096]{2,1,0:T(8,128)(2,1)}, ...), branch_computations={%region_1.1_spmd, %region_2.2_spmd} | conditional | flops 272629760 | bytes 17892492 | solution.py:80
  114.0 7.8 %select_add_fusion = (f32[256,4096]{1,0:T(8,128)}, f32[256,4096]{1,0:T(8,128)}) fusion(f32[256,4096]{1,0:T(8,128)} %get-tuple-element.269, pred[]{:T(512)} %get-tuple-element.270, f32[256,4096]{1,0:T(8,128)} %get-tuple-element.263, pred[]{:T(512)} %get-tuple-element.264, bf16[9,128,4096]{2,1,0:T(8,128)(2,1)} %get-tuple-element.267, s32[]{:T(128)S(6)} %min.21, ...), kind=kOutput, calls=%fused_computation.1 | convolution fusion | flops 272629760 | bytes 17892360 | tf_op jit(solution)/shard_map/while/body/eval_jaxpr/cond/branch_1_fun/dot_general | solution.py:71
  121.8 7.8 %conditional.2 = ((f32[256,4096]{1,0:T(8,128)}, f32[256,4096]{1,0:T(8,128)})) conditional(s32[]{:T(128)} %convert_element_type.30, (f32[256,4096]{1,0:T(8,128)}, f32[256,4096]{1,0:T(8,128)}) %tuple.62, (pred[]{:T(512)}, s32[]{:T(128)}, bf16[16,256,128]{2,1,0:T(8,128)(2,1)S(1)}, s32[]{:T(128)}, bf16[9,128,4096]{2,1,0:T(8,128)(2,1)}, ...), branch_computations={%region_1.1_spmd, %region_2.2_spmd} | conditional | flops 272629760 | bytes 17892492 | solution.py:80
  121.8 7.8 %select_add_fusion = (f32[256,4096]{1,0:T(8,128)}, f32[256,4096]{1,0:T(8,128)}) fusion(f32[256,4096]{1,0:T(8,128)} %get-tuple-element.269, pred[]{:T(512)} %get-tuple-element.270, f32[256,4096]{1,0:T(8,128)} %get-tuple-element.263, pred[]{:T(512)} %get-tuple-element.264, bf16[9,128,4096]{2,1,0:T(8,128)(2,1)} %get-tuple-element.267, s32[]{:T(128)S(6)} %min.21, ...), kind=kOutput, calls=%fused_computation.1 | convolution fusion | flops 272629760 | bytes 17892360 | tf_op jit(solution)/shard_map/while/body/eval_jaxpr/cond/branch_1_fun/dot_general | solution.py:71
  129.7 7.8 %conditional.2 = ((f32[256,4096]{1,0:T(8,128)}, f32[256,4096]{1,0:T(8,128)})) conditional(s32[]{:T(128)} %convert_element_type.30, (f32[256,4096]{1,0:T(8,128)}, f32[256,4096]{1,0:T(8,128)}) %tuple.62, (pred[]{:T(512)}, s32[]{:T(128)}, bf16[16,256,128]{2,1,0:T(8,128)(2,1)S(1)}, s32[]{:T(128)}, bf16[9,128,4096]{2,1,0:T(8,128)(2,1)}, ...), branch_computations={%region_1.1_spmd, %region_2.2_spmd} | conditional | flops 272629760 | bytes 17892492 | solution.py:80
  129.7 7.8 %select_add_fusion = (f32[256,4096]{1,0:T(8,128)}, f32[256,4096]{1,0:T(8,128)}) fusion(f32[256,4096]{1,0:T(8,128)} %get-tuple-element.269, pred[]{:T(512)} %get-tuple-element.270, f32[256,4096]{1,0:T(8,128)} %get-tuple-element.263, pred[]{:T(512)} %get-tuple-element.264, bf16[9,128,4096]{2,1,0:T(8,128)(2,1)} %get-tuple-element.267, s32[]{:T(128)S(6)} %min.21, ...), kind=kOutput, calls=%fused_computation.1 | convolution fusion | flops 272629760 | bytes 17892360 | tf_op jit(solution)/shard_map/while/body/eval_jaxpr/cond/branch_1_fun/dot_general | solution.py:71
  137.5 7.8 %conditional.2 = ((f32[256,4096]{1,0:T(8,128)}, f32[256,4096]{1,0:T(8,128)})) conditional(s32[]{:T(128)} %convert_element_type.30, (f32[256,4096]{1,0:T(8,128)}, f32[256,4096]{1,0:T(8,128)}) %tuple.62, (pred[]{:T(512)}, s32[]{:T(128)}, bf16[16,256,128]{2,1,0:T(8,128)(2,1)S(1)}, s32[]{:T(128)}, bf16[9,128,4096]{2,1,0:T(8,128)(2,1)}, ...), branch_computations={%region_1.1_spmd, %region_2.2_spmd} | conditional | flops 272629760 | bytes 17892492 | solution.py:80
  137.5 7.8 %select_add_fusion = (f32[256,4096]{1,0:T(8,128)}, f32[256,4096]{1,0:T(8,128)}) fusion(f32[256,4096]{1,0:T(8,128)} %get-tuple-element.269, pred[]{:T(512)} %get-tuple-element.270, f32[256,4096]{1,0:T(8,128)} %get-tuple-element.263, pred[]{:T(512)} %get-tuple-element.264, bf16[9,128,4096]{2,1,0:T(8,128)(2,1)} %get-tuple-element.267, s32[]{:T(128)S(6)} %min.21, ...), kind=kOutput, calls=%fused_computation.1 | convolution fusion | flops 272629760 | bytes 17892360 | tf_op jit(solution)/shard_map/while/body/eval_jaxpr/cond/branch_1_fun/dot_general | solution.py:71
  145.3 7.8 %conditional.2 = ((f32[256,4096]{1,0:T(8,128)}, f32[256,4096]{1,0:T(8,128)})) conditional(s32[]{:T(128)} %convert_element_type.30, (f32[256,4096]{1,0:T(8,128)}, f32[256,4096]{1,0:T(8,128)}) %tuple.62, (pred[]{:T(512)}, s32[]{:T(128)}, bf16[16,256,128]{2,1,0:T(8,128)(2,1)S(1)}, s32[]{:T(128)}, bf16[9,128,4096]{2,1,0:T(8,128)(2,1)}, ...), branch_computations={%region_1.1_spmd, %region_2.2_spmd} | conditional | flops 272629760 | bytes 17892492 | solution.py:80
  145.3 7.8 %select_add_fusion = (f32[256,4096]{1,0:T(8,128)}, f32[256,4096]{1,0:T(8,128)}) fusion(f32[256,4096]{1,0:T(8,128)} %get-tuple-element.269, pred[]{:T(512)} %get-tuple-element.270, f32[256,4096]{1,0:T(8,128)} %get-tuple-element.263, pred[]{:T(512)} %get-tuple-element.264, bf16[9,128,4096]{2,1,0:T(8,128)(2,1)} %get-tuple-element.267, s32[]{:T(128)S(6)} %min.21, ...), kind=kOutput, calls=%fused_computation.1 | convolution fusion | flops 272629760 | bytes 17892360 | tf_op jit(solution)/shard_map/while/body/eval_jaxpr/cond/branch_1_fun/dot_general | solution.py:71
  153.1 7.8 %conditional.2 = ((f32[256,4096]{1,0:T(8,128)}, f32[256,4096]{1,0:T(8,128)})) conditional(s32[]{:T(128)} %convert_element_type.30, (f32[256,4096]{1,0:T(8,128)}, f32[256,4096]{1,0:T(8,128)}) %tuple.62, (pred[]{:T(512)}, s32[]{:T(128)}, bf16[16,256,128]{2,1,0:T(8,128)(2,1)S(1)}, s32[]{:T(128)}, bf16[9,128,4096]{2,1,0:T(8,128)(2,1)}, ...), branch_computations={%region_1.1_spmd, %region_2.2_spmd} | conditional | flops 272629760 | bytes 17892492 | solution.py:80
  153.1 7.8 %select_add_fusion = (f32[256,4096]{1,0:T(8,128)}, f32[256,4096]{1,0:T(8,128)}) fusion(f32[256,4096]{1,0:T(8,128)} %get-tuple-element.269, pred[]{:T(512)} %get-tuple-element.270, f32[256,4096]{1,0:T(8,128)} %get-tuple-element.263, pred[]{:T(512)} %get-tuple-element.264, bf16[9,128,4096]{2,1,0:T(8,128)(2,1)} %get-tuple-element.267, s32[]{:T(128)S(6)} %min.21, ...), kind=kOutput, calls=%fused_computation.1 | convolution fusion | flops 272629760 | bytes 17892360 | tf_op jit(solution)/shard_map/while/body/eval_jaxpr/cond/branch_1_fun/dot_general | solution.py:71
  161.0 7.8 %conditional.2 = ((f32[256,4096]{1,0:T(8,128)}, f32[256,4096]{1,0:T(8,128)})) conditional(s32[]{:T(128)} %convert_element_type.30, (f32[256,4096]{1,0:T(8,128)}, f32[256,4096]{1,0:T(8,128)}) %tuple.62, (pred[]{:T(512)}, s32[]{:T(128)}, bf16[16,256,128]{2,1,0:T(8,128)(2,1)S(1)}, s32[]{:T(128)}, bf16[9,128,4096]{2,1,0:T(8,128)(2,1)}, ...), branch_computations={%region_1.1_spmd, %region_2.2_spmd} | conditional | flops 272629760 | bytes 17892492 | solution.py:80
  161.0 7.8 %select_add_fusion = (f32[256,4096]{1,0:T(8,128)}, f32[256,4096]{1,0:T(8,128)}) fusion(f32[256,4096]{1,0:T(8,128)} %get-tuple-element.269, pred[]{:T(512)} %get-tuple-element.270, f32[256,4096]{1,0:T(8,128)} %get-tuple-element.263, pred[]{:T(512)} %get-tuple-element.264, bf16[9,128,4096]{2,1,0:T(8,128)(2,1)} %get-tuple-element.267, s32[]{:T(128)S(6)} %min.21, ...), kind=kOutput, calls=%fused_computation.1 | convolution fusion | flops 272629760 | bytes 17892360 | tf_op jit(solution)/shard_map/while/body/eval_jaxpr/cond/branch_1_fun/dot_general | solution.py:71
  168.8 0.0 reduce-scatter.9.cloned.1.call-update
  168.8 0.0 reduce-scatter.11.cloned.1.call-start
  168.9 49.9 %reduce-scatter.9.cloned.1.call-done = f32[256,512]{1,0:T(8,128)} async-done(((f32[256,4096]{1,0:T(8,128)}), f32[256,512]{1,0:T(8,128)}) %reduce-scatter.9.cloned.1.call-update) | async-done | bytes 524304 | tf_op jit(solution)/shard_map/reduce_scatter | solution.py:28
  218.8 0.0 reduce-scatter.11.cloned.1.call-update
  218.8 0.0 reduce-scatter.5.cloned.1.call-start
  218.8 0.7 reduce-scatter.5.cloned.1.call-update
  219.5 0.0 reduce-scatter.7.cloned.1.call-start
  219.6 18.9 %reduce-scatter.11.cloned.1.call-done = f32[256,256]{1,0:T(8,128)} async-done(((f32[256,512]{1,0:T(8,128)}), f32[256,256]{1,0:T(8,128)}) %reduce-scatter.11.cloned.1.call-update) | async-done | bytes 262160 | tf_op jit(solution)/shard_map/reduce_scatter | solution.py:28
  238.5 60.0 %reduce-scatter.5.cloned.1.call-done = f32[256,512]{1,0:T(8,128)} async-done(((f32[256,4096]{1,0:T(8,128)}), f32[256,512]{1,0:T(8,128)}) %reduce-scatter.5.cloned.1.call-update) | async-done | bytes 524304 | tf_op jit(solution)/shard_map/reduce_scatter | solution.py:28
  298.5 0.0 reduce-scatter.7.cloned.1.call-update
  298.6 0.0 all-gather.2.cloned.1.call-start
  298.6 2.2 collective-permute-start.1
  300.8 7.4 %collective-permute-done.1 = f32[256,256]{1,0:T(8,128)S(1)} collective-permute-done((f32[256,256]{1,0:T(8,128)S(1)}, f32[256,256]{1,0:T(8,128)S(1)}, u32[]{:S(2)}, u32[]{:S(2)}) %collective-permute-start.1) | collective-permute-done | bytes 262176 | tf_op jit(solution)/shard_map/ppermute | solution.py:33
  308.2 1.5 collective-permute-start.2
  309.7 5.6 %collective-permute-done.2 = f32[256,256]{1,0:T(8,128)S(1)} collective-permute-done((f32[256,256]{1,0:T(8,128)S(1)}, f32[256,256]{1,0:T(8,128)S(1)}, u32[]{:S(2)}, u32[]{:S(2)}) %collective-permute-start.2) | collective-permute-done | bytes 262176 | tf_op jit(solution)/shard_map/ppermute | solution.py:33
  315.3 3.0 collective-permute-start.3
  318.3 0.7 constant_dynamic-slice_fusion
  319.0 4.2 collective-permute-done.3
  323.2 1.0 fusion.16
  324.2 0.1 collective-permute-start.4
  324.3 1.3 collective-permute-done.4
  325.7 2.1 collective-permute-start.5
  327.8 5.0 collective-permute-done.5
  332.7 1.5 collective-permute-start.6
  334.2 3.5 collective-permute-done.6
  337.7 3.0 collective-permute-start.7
  340.7 3.5 collective-permute-done.7
  344.1 0.7 pad_maximum_fusion
  345.0 118.1 %all-gather.2.cloned.1.call-done = bf16[512,4096]{1,0:T(8,128)(2,1)} async-done(((bf16[512,256]{1,0:T(8,128)(2,1)}), bf16[512,4096]{1,0:T(8,128)(2,1)}) %all-gather.2.cloned.1.call-update) | async-done | bytes 4194320 | tf_op jit(solution)/shard_map/all_gather | solution.py:38
  463.1 2.7 fusion.21
  465.8 8.8 %fusion.6 = f32[9,256,128]{2,1,0:T(8,128)} fusion(pred[9]{0:T(512)(128)(4,1)S(1)} %iota_compare_fusion, bf16[256,4096]{1,0:T(8,128)(2,1)S(1)} %get-tuple-element.307, bf16[256,4096]{1,0:T(8,128)(2,1)S(1)} %get-tuple-element.306, bf16[1,9,128,4096]{3,2,1,0:T(8,128)(2,1)} %bitcast.41), kind=kOutput, calls=%fused_computation.9 | convolution fusion | flops 2425356288 | bytes 14811145 | tf_op jit(solution)/shard_map/jtd,jfd->jtf/dot_general | solution.py:125
  474.6 1.9 gather_fusion
  476.6 0.3 fusion.12
  476.9 37.9 %all_to_all.16 = f32[16,1,256,128]{3,2,1,0:T(8,128)S(1)} all-to-all(f32[16,1,256,128]{3,2,1,0:T(8,128)S(1)} %fusion.12), channel_id=1, replica_groups=mesh['layer'=16,'feat_0'=8,'feat_1'=2] {'layer'}, dimensions={0} | all-to-all | bytes 4194304 | tf_op jit(solution)/shard_map/all_to_all | solution.py:52
  514.8 0.8 reduce_sum.11
  (23 shorter events, 0.1 us)
Async XLA Ops:
  7.2 60.0 %copy-start = (bf16[1,4096,128]{2,1,0:T(8,128)(2,1)S(1)}, bf16[1,4096,128]{2,1,0:T(8,128)(2,1)}, u32[]{:S(2)}) copy-start(bf16[1,4096,128]{2,1,0:T(8,128)(2,1)} %param.12) | copy-start | bytes 3145732
  7.2 60.0 %copy-start.3 = (f32[1,128]{1,0:T(1,128)S(1)}, f32[1,128]{1,0:T(1,128)}, u32[]{:S(2)}) copy-start(f32[1,128]{1,0:T(1,128)} %param.13) | copy-start | bytes 1540
  69.1 24.2 %all-to-all-start.1 = ((bf16[16,1,256,128]{3,2,1,0:T(8,128)(2,1)}), bf16[16,1,256,128]{3,2,1,0:T(8,128)(2,1)S(1)}, u32[]{:S(2)}, u32[]{:S(2)}) async-start(bf16[16,1,256,128]{3,2,1,0:T(8,128)(2,1)} %broadcast_in_dim.69), calls=%async_computation.1 | async-start | bytes 2097152 | tf_op jit(solution)/shard_map/all_to_all | solution.py:12
  75.3 143.5 %reduce-scatter.9.cloned.1.call-start = ((), (), s32[]{:S(2)}) async-start(), calls=%async_computation.9 | async-start | bytes 4718592 | tf_op jit(solution)/shard_map/reduce_scatter | solution.py:28
  168.8 154.4 %copy-start.2 = (bf16[1,256,256]{2,1,0:T(8,128)(2,1)S(1)}, bf16[1,256,256]{2,1,0:T(8,128)(2,1)}, u32[]{:S(2)}) copy-start(bf16[1,256,256]{2,1,0:T(8,128)(2,1)} %param.11) | copy-start | bytes 393220
  168.8 69.7 %reduce-scatter.11.cloned.1.call-start = ((), (), s32[]{:S(2)}) async-start(), calls=%async_computation.10 | async-start | bytes 786432 | tf_op jit(solution)/shard_map/reduce_scatter | solution.py:28
  218.8 79.7 %reduce-scatter.5.cloned.1.call-start = ((), (), s32[]{:S(2)}) async-start(), calls=%async_computation.7 | async-start | bytes 4718592 | tf_op jit(solution)/shard_map/reduce_scatter | solution.py:28
  219.5 99.5 %reduce-scatter.7.cloned.1.call-start = ((), (), s32[]{:S(2)}) async-start(), calls=%async_computation.8 | async-start | bytes 786432 | tf_op jit(solution)/shard_map/reduce_scatter | solution.py:28
  238.5 60.1 %collective-permute-start = (f32[256,256]{1,0:T(8,128)}, f32[256,256]{1,0:T(8,128)S(1)}, u32[]{:S(2)}, u32[]{:S(2)}) collective-permute-start(f32[256,256]{1,0:T(8,128)} %reduce-scatter.11.cloned.1.call-done), channel_id=1, source_target_pairs={{0,16},{16,0},{32,48},{48,32},{64,80},{80,64},{96,112},{112,96},{1... | collective-permute-start | bytes 786440 | tf_op jit(solution)/shard_map/ppermute | solution.py:33
  298.6 164.5 %all-gather.2.cloned.1.call-start = ((), (), s32[]{:S(2)}) async-start(), calls=%async_computation.11 | async-start | bytes 4456448 | tf_op jit(solution)/shard_map/all_gather | solution.py:38
  298.6 9.6 %collective-permute-start.1 = (f32[256,256]{1,0:T(8,128)S(1)}, f32[256,256]{1,0:T(8,128)S(1)}, u32[]{:S(2)}, u32[]{:S(2)}) collective-permute-start(f32[256,256]{1,0:T(8,128)S(1)} %collective-permute-done), channel_id=1, source_target_pairs={{0,32},{16,48},{32,0},{48,16},{64,96},{80,112},{96,64},{112,80},{1... | collective-permute-start | bytes 786440 | tf_op jit(solution)/shard_map/ppermute | solution.py:33
  308.2 7.1 %collective-permute-start.2 = (f32[256,256]{1,0:T(8,128)S(1)}, f32[256,256]{1,0:T(8,128)S(1)}, u32[]{:S(2)}, u32[]{:S(2)}) collective-permute-start(f32[256,256]{1,0:T(8,128)S(1)} %collective-permute-done.1), channel_id=1, source_target_pairs={{0,64},{16,80},{32,96},{48,112},{64,0},{80,16},{96,32},{112,48},{1... | collective-permute-start | bytes 786440 | tf_op jit(solution)/shard_map/ppermute | solution.py:33
  315.3 7.9 %collective-permute-start.3 = (f32[256,256]{1,0:T(8,128)S(1)}, f32[256,256]{1,0:T(8,128)S(1)}, u32[]{:S(2)}, u32[]{:S(2)}) collective-permute-start(f32[256,256]{1,0:T(8,128)S(1)} %collective-permute-done.2), channel_id=1, source_target_pairs={{0,128},{16,144},{32,160},{48,176},{64,192},{80,208},{96,224},{112... | collective-permute-start | bytes 786440 | tf_op jit(solution)/shard_map/ppermute | solution.py:33
  324.2 141.6 %copy-start.1 = (bf16[256,256]{1,0:T(8,128)(2,1)}, bf16[256,256]{1,0:T(8,128)(2,1)S(1)}, u32[]{:S(2)}) copy-start(bf16[256,256]{1,0:T(8,128)(2,1)S(1)} %fusion.16) | copy-start | bytes 393220
  324.2 1.4 collective-permute-start.4
  325.7 7.1 %collective-permute-start.5 = (bf16[256,256]{1,0:T(8,128)(2,1)S(1)}, bf16[256,256]{1,0:T(8,128)(2,1)S(1)}, u32[]{:S(2)}, u32[]{:S(2)}) collective-permute-start(bf16[256,256]{1,0:T(8,128)(2,1)S(1)} %collective-permute-done.4), channel_id=1, source_target_pairs={{0,32},{16,48},{32,0},{48,16},{64,96},{80,112},{96,64},{112,80},{1... | collective-permute-start | bytes 393224 | tf_op jit(solution)/shard_map/ppermute | solution.py:33
  332.7 5.0 collective-permute-start.6
  337.7 6.5 %collective-permute-start.7 = (bf16[256,256]{1,0:T(8,128)(2,1)S(1)}, bf16[256,256]{1,0:T(8,128)(2,1)S(1)}, u32[]{:S(2)}, u32[]{:S(2)}) collective-permute-start(bf16[256,256]{1,0:T(8,128)(2,1)S(1)} %collective-permute-done.6), channel_id=1, source_target_pairs={{0,128},{16,144},{32,160},{48,176},{64,192},{80,208},{96,224},{112... | collective-permute-start | bytes 393224 | tf_op jit(solution)/shard_map/ppermute | solution.py:33
Sparse Core Ops, SparseCore 0:
  168.9 49.7 reduce-scatter.8
  221.3 17.2 reduce-scatter.10
  241.1 57.4 reduce-scatter.4
  300.9 17.2 reduce-scatter.6
  345.0 117.9 all-gather.1
